TPU v7x, 32 devices: a whole 2x2x4 slice. The times are simulated.
32 devices in a mesh: section: 4 (over y, x), tensor: 8 (over z, core).
Axes of the slice: x: 2, y: 2, z: 4, core: 2. Of those that a mesh axis runs over, the one named last changes fastest.
Arguments:
- tokens: bfloat16 [2, 32, 4096], P(None, 'tensor'), may hold values from -24 to 24
- expert_ids: int32 [4, 2, 32, 2], P('section', None, 'tensor'), may hold values from 0 to 7, as said below
- router_weight: bfloat16 [4, 4096, 8], P('section'), may hold values from -0.09375 to 0.09375
- norm_gain: float32 [4, 4096], P('section'), may hold values from 0.1 to 1.9
- gate_weight: bfloat16 [4, 28672, 4096], P('section', 'tensor'), may hold values from -0.09375 to 0.09375
- up_weight: bfloat16 [4, 28672, 4096], P('section', 'tensor'), may hold values from -0.09375 to 0.09375
- down_weight: bfloat16 [4, 28672, 4096], P('section', 'tensor'), may hold values from -0.046875 to 0.046875
Outputs:
- section_outputs: bfloat16 [4, 2, 32, 4096], P('section', None, 'tensor')
Inputs may be any that keep to these rules, and one draw needn't show every extreme that they name: `expert_ids`: each token names two different experts. Along the token dimension, in aligned blocks of 4 tokens of one micro-batch and one layer, at most 2 tokens name expert 0 and at most 2 name expert 1; in some micro-batch of every layer every block has exactly 2 of each.
All inputs are finite; a program needn't handle non-finite values.
Results may differ from a plain program's by a relative error of at most 0.0055.
Values may be sent and summed in bfloat16 or wider, within the bound.
No kernel may reach another device: no remote copies, remote signals or barrier semaphores. Data moves between devices by JAX's collectives and lax.ppermute only.
A program may use at most 128 MiB of HBM per device.

v0:
```python
import jax
import jax.numpy as jnp
from jax import lax
from jax.sharding import PartitionSpec as P

EPSILON = 1e-05


def from_behind(block, axis, distance):
    devices = range(lax.axis_size(axis))
    route = [(i - distance, i) for i in devices if i - distance in devices]
    return lax.ppermute(block, axis, route)


def normalize(hidden_rows, gain):
    wide = hidden_rows.astype(jnp.float32)
    scale = lax.rsqrt(jnp.mean(wide * wide, axis=-1, keepdims=True) + EPSILON)
    return (wide * scale * gain).astype(jnp.bfloat16)


def mixing_weight(logits, routes, expert):
    routed = (routes[:, 0] == expert) | (routes[:, 1] == expert)
    partner = jnp.where(routes[:, 0] == expert, routes[:, 1], routes[:, 0])
    columns = lax.broadcasted_iota(jnp.int32, logits.shape, 1)
    partner_logit = jnp.sum(jnp.where(columns == partner[:, None], logits, 0.0), axis=1)
    value = 1.0 / (1.0 + jnp.exp(partner_logit - logits[:, expert]))
    return (jnp.where(routed, value, 0.0), routed.astype(jnp.int32))


def pickers(flags, slot_count):
    place = jnp.cumsum(flags, axis=1) - 1
    slots = lax.broadcasted_iota(jnp.int32, (1, slot_count, 1), 1)
    chosen = (place[:, None, :] == slots) & (flags[:, None, :] == 1)
    return chosen.astype(jnp.float32)


def project_rows(rows, weight_rows):
    return lax.dot_general(
        rows, weight_rows, (((1,), (1,)), ((), ())), preferred_element_type=jnp.float32
    )


def body(tokens, expert_ids, router_weight, norm_gain, gate_weight, up_weight, down_weight):
    sections = lax.axis_size("section")
    section = lax.axis_index("section")
    group = lax.axis_index("tensor") // (lax.axis_size("tensor") // 2)
    micro, count, width = tokens.shape
    slot_count = count // 2
    router = router_weight[0]
    gain = norm_gain[0]
    w_gate = gate_weight[0]
    w_up = up_weight[0]
    w_down = down_weight[0]
    all_routes = expert_ids[0]

    def expand(piece):
        gate = project_rows(piece, w_gate)
        upward = project_rows(piece, w_up)
        return (jax.nn.silu(gate) * upward).astype(jnp.bfloat16)

    def own_expert(piece):
        return expand(lax.dynamic_index_in_dim(piece, group, 0, keepdims=False))

    def layer(hidden_rows, routes):
        normed = normalize(hidden_rows, gain)
        logits = jnp.dot(normed, router, preferred_element_type=jnp.float32)
        weight_zero, flags_zero = mixing_weight(logits, routes, 0)
        weight_one, flags_one = mixing_weight(logits, routes, 1)
        pick_zero = pickers(flags_zero[None, :], slot_count)[0]
        pick_one = pickers(flags_one[None, :], slot_count)[0]
        both_picks = jnp.stack([pick_zero, pick_one]).astype(jnp.bfloat16)
        mine = jnp.einsum(
            "esj,jd->esd", both_picks, normed, preferred_element_type=jnp.float32
        ).astype(jnp.bfloat16)
        hidden = own_expert(lax.all_gather(mine, "tensor", axis=1, tiled=True))
        product = jnp.dot(hidden, w_down, preferred_element_type=jnp.float32)
        product = product.reshape(
            2 * slot_count * lax.axis_size("tensor") // (2 * slot_count), 1, slot_count, width
        )
        which = lax.broadcasted_iota(jnp.int32, (1, 2, 1, 1), 1)
        term = jnp.where(which == group, product, 0.0)
        summed = lax.psum_scatter(
            term.reshape(2 * slot_count * lax.axis_size("tensor"), width),
            "tensor",
            scatter_dimension=0,
            tiled=True,
        )
        expert_zero = jnp.dot(pick_zero.T, summed[:slot_count], precision=lax.Precision.HIGHEST)
        expert_one = jnp.dot(pick_one.T, summed[slot_count:], precision=lax.Precision.HIGHEST)
        total = (
            hidden_rows.astype(jnp.float32)
            + weight_zero[:, None] * expert_zero
            + weight_one[:, None] * expert_one
        )
        return total.astype(jnp.bfloat16)

    def advance(step, carry):
        incoming, stash = carry
        number = step - section
        active = (number >= 0) & (number < micro)
        position = jnp.clip(number, 0, micro - 1)
        fresh = lax.dynamic_index_in_dim(tokens, position, 0, keepdims=False)
        current = jnp.where(section == 0, fresh, incoming)
        routes = lax.dynamic_index_in_dim(all_routes, position, 0, keepdims=False)
        result = layer(current, routes)
        before = lax.dynamic_index_in_dim(stash, position, 0, keepdims=False)
        stash = lax.dynamic_update_index_in_dim(
            stash, jnp.where(active, result, before), position, 0
        )
        incoming = from_behind(result, "section", 1)
        return (incoming, stash)

    initial = (jnp.zeros((count, width), jnp.bfloat16), jnp.zeros_like(tokens))
    final_pass, stash = lax.fori_loop(0, micro + sections - 1, advance, initial)
    return stash[None]


def solution(mesh):
    return jax.shard_map(
        body,
        mesh=mesh,
        in_specs=(
            P(None, "tensor", None),
            P("section", None, "tensor", None),
            P("section", None, None),
            P("section", None),
            P("section", "tensor", None),
            P("section", "tensor", None),
            P("section", "tensor", None),
        ),
        out_specs=P("section", None, "tensor", None),
        check_vma=False,
    )
```

profile of v0, /device:TPU:6, one launch (start us, length us, event | category | flops | bytes accessed | tf_op | source)
XLA Modules:
  0.0 617.6 jit_solution(7769537876816631305)
XLA Ops:
  6.6 603.8 %while.18 = (s32[]{:T(128)}, bf16[4,4096]{1,0:T(4,128)(2,1)S(1)}, bf16[2,4,4096]{2,1,0:T(4,128)(2,1)S(1)}, pred[]{:T(512)}, s32[]{:T(128)}, /*index=5*/bf16[2,4,...) while((s32[]{:T(128)}, bf16[4,4096]{1,0:T(4,128)(2,1)S(1)}, ...), condition=%wide.region_7.8_spmd, body=%wide.region_0.7_spmd.sunk | while | flops 1411334528 | bytes 97111616 | solution.py:114
  11.6 14.4 %all_gather.12 = bf16[2,16,4096]{2,0,1:T(2,128)(2,1)S(1)} all-gather(bf16[2,2,4096]{2,0,1:T(2,128)(2,1)S(1)} %copy.47), channel_id=1, replica_groups=mesh['section'=4,'tensor'=8] {'tensor'}, dimensions={1}, use_global_device_ids=true | all-gather | bytes 294912 | tf_op jit(solution)/shard_map/while/body/eval_jaxpr/all_gather | solution.py:75
  26.4 13.2 %fusion.82 = f32[16,3584]{1,0:T(8,128)S(1)} fusion(bf16[3584,4096]{1,0:T(8,128)(2,1)} %get-tuple-element.569, bf16[1,16,4096]{2,0,1:T(2,128)(2,1)S(1)} %constant_dynamic-slice_fusion.6), kind=kOutput, calls=%fused_computation.22.clone.1 | convolution fusion | flops 469762048 | bytes 29720576 | tf_op jit(solution)/shard_map/while/body/eval_jaxpr/dot_general | solution.py:38
  39.6 21.8 %fusion.83 = f32[16,4096]{1,0:T(8,128)S(1)} fusion(bf16[3584,4096]{1,0:T(8,128)(2,1)} %get-tuple-element.571, bf16[3584,4096]{1,0:T(8,128)(2,1)} %get-tuple-element.570, f32[16,3584]{1,0:T(8,128)S(1)} %fusion.82, bf16[1,16,4096]{2,0,1:T(2,128)(2,1)S(1)} %constant_dynamic-slice_fusion.6), kind=kOutput, calls=%fused_computation.8.clone.1 | convolution fusion | flops 939868160 | bytes 59342848 | tf_op jit(solution)/shard_map/while/body/eval_jaxpr/dot_general | solution.py:76
  64.5 56.5 %all-reduce.5.cloned.1.call-done = f32[32,4096]{1,0:T(8,128)} async-done(((f32[32,4096]{1,0:T(8,128)}), f32[32,4096]{1,0:T(8,128)}) %all-reduce.5.cloned.1.call-update) | async-done | bytes 524304 | tf_op jit(solution)/shard_map/while
  124.7 4.5 collective-permute-done
  134.2 14.2 %all_gather.12 = bf16[2,16,4096]{2,0,1:T(2,128)(2,1)S(1)} all-gather(bf16[2,2,4096]{2,0,1:T(2,128)(2,1)S(1)} %copy.47), channel_id=1, replica_groups=mesh['section'=4,'tensor'=8] {'tensor'}, dimensions={1}, use_global_device_ids=true | all-gather | bytes 294912 | tf_op jit(solution)/shard_map/while/body/eval_jaxpr/all_gather | solution.py:75
  148.7 13.2 %fusion.82 = f32[16,3584]{1,0:T(8,128)S(1)} fusion(bf16[3584,4096]{1,0:T(8,128)(2,1)} %get-tuple-element.569, bf16[1,16,4096]{2,0,1:T(2,128)(2,1)S(1)} %constant_dynamic-slice_fusion.6), kind=kOutput, calls=%fused_computation.22.clone.1 | convolution fusion | flops 469762048 | bytes 29720576 | tf_op jit(solution)/shard_map/while/body/eval_jaxpr/dot_general | solution.py:38
  162.0 21.8 %fusion.83 = f32[16,4096]{1,0:T(8,128)S(1)} fusion(bf16[3584,4096]{1,0:T(8,128)(2,1)} %get-tuple-element.571, bf16[3584,4096]{1,0:T(8,128)(2,1)} %get-tuple-element.570, f32[16,3584]{1,0:T(8,128)S(1)} %fusion.82, bf16[1,16,4096]{2,0,1:T(2,128)(2,1)S(1)} %constant_dynamic-slice_fusion.6), kind=kOutput, calls=%fused_computation.8.clone.1 | convolution fusion | flops 939868160 | bytes 59342848 | tf_op jit(solution)/shard_map/while/body/eval_jaxpr/dot_general | solution.py:76
  186.9 54.4 %all-reduce.5.cloned.1.call-done = f32[32,4096]{1,0:T(8,128)} async-done(((f32[32,4096]{1,0:T(8,128)}), f32[32,4096]{1,0:T(8,128)}) %all-reduce.5.cloned.1.call-update) | async-done | bytes 524304 | tf_op jit(solution)/shard_map/while
  245.0 4.5 collective-permute-done
  254.5 14.2 %all_gather.12 = bf16[2,16,4096]{2,0,1:T(2,128)(2,1)S(1)} all-gather(bf16[2,2,4096]{2,0,1:T(2,128)(2,1)S(1)} %copy.47), channel_id=1, replica_groups=mesh['section'=4,'tensor'=8] {'tensor'}, dimensions={1}, use_global_device_ids=true | all-gather | bytes 294912 | tf_op jit(solution)/shard_map/while/body/eval_jaxpr/all_gather | solution.py:75
  269.0 13.2 %fusion.82 = f32[16,3584]{1,0:T(8,128)S(1)} fusion(bf16[3584,4096]{1,0:T(8,128)(2,1)} %get-tuple-element.569, bf16[1,16,4096]{2,0,1:T(2,128)(2,1)S(1)} %constant_dynamic-slice_fusion.6), kind=kOutput, calls=%fused_computation.22.clone.1 | convolution fusion | flops 469762048 | bytes 29720576 | tf_op jit(solution)/shard_map/while/body/eval_jaxpr/dot_general | solution.py:38
  282.3 21.8 %fusion.83 = f32[16,4096]{1,0:T(8,128)S(1)} fusion(bf16[3584,4096]{1,0:T(8,128)(2,1)} %get-tuple-element.571, bf16[3584,4096]{1,0:T(8,128)(2,1)} %get-tuple-element.570, f32[16,3584]{1,0:T(8,128)S(1)} %fusion.82, bf16[1,16,4096]{2,0,1:T(2,128)(2,1)S(1)} %constant_dynamic-slice_fusion.6), kind=kOutput, calls=%fused_computation.8.clone.1 | convolution fusion | flops 939868160 | bytes 59342848 | tf_op jit(solution)/shard_map/while/body/eval_jaxpr/dot_general | solution.py:76
  307.1 54.4 %all-reduce.5.cloned.1.call-done = f32[32,4096]{1,0:T(8,128)} async-done(((f32[32,4096]{1,0:T(8,128)}), f32[32,4096]{1,0:T(8,128)}) %all-reduce.5.cloned.1.call-update) | async-done | bytes 524304 | tf_op jit(solution)/shard_map/while
  365.3 4.5 collective-permute-done
  374.8 14.2 %all_gather.12 = bf16[2,16,4096]{2,0,1:T(2,128)(2,1)S(1)} all-gather(bf16[2,2,4096]{2,0,1:T(2,128)(2,1)S(1)} %copy.47), channel_id=1, replica_groups=mesh['section'=4,'tensor'=8] {'tensor'}, dimensions={1}, use_global_device_ids=true | all-gather | bytes 294912 | tf_op jit(solution)/shard_map/while/body/eval_jaxpr/all_gather | solution.py:75
  389.3 13.2 %fusion.82 = f32[16,3584]{1,0:T(8,128)S(1)} fusion(bf16[3584,4096]{1,0:T(8,128)(2,1)} %get-tuple-element.569, bf16[1,16,4096]{2,0,1:T(2,128)(2,1)S(1)} %constant_dynamic-slice_fusion.6), kind=kOutput, calls=%fused_computation.22.clone.1 | convolution fusion | flops 469762048 | bytes 29720576 | tf_op jit(solution)/shard_map/while/body/eval_jaxpr/dot_general | solution.py:38
  402.5 21.8 %fusion.83 = f32[16,4096]{1,0:T(8,128)S(1)} fusion(bf16[3584,4096]{1,0:T(8,128)(2,1)} %get-tuple-element.571, bf16[3584,4096]{1,0:T(8,128)(2,1)} %get-tuple-element.570, f32[16,3584]{1,0:T(8,128)S(1)} %fusion.82, bf16[1,16,4096]{2,0,1:T(2,128)(2,1)S(1)} %constant_dynamic-slice_fusion.6), kind=kOutput, calls=%fused_computation.8.clone.1 | convolution fusion | flops 939868160 | bytes 59342848 | tf_op jit(solution)/shard_map/while/body/eval_jaxpr/dot_general | solution.py:76
  427.4 54.4 %all-reduce.5.cloned.1.call-done = f32[32,4096]{1,0:T(8,128)} async-done(((f32[32,4096]{1,0:T(8,128)}), f32[32,4096]{1,0:T(8,128)}) %all-reduce.5.cloned.1.call-update) | async-done | bytes 524304 | tf_op jit(solution)/shard_map/while
  495.1 14.2 %all_gather.12 = bf16[2,16,4096]{2,0,1:T(2,128)(2,1)S(1)} all-gather(bf16[2,2,4096]{2,0,1:T(2,128)(2,1)S(1)} %copy.47), channel_id=1, replica_groups=mesh['section'=4,'tensor'=8] {'tensor'}, dimensions={1}, use_global_device_ids=true | all-gather | bytes 294912 | tf_op jit(solution)/shard_map/while/body/eval_jaxpr/all_gather | solution.py:75
  509.6 13.2 %fusion.82 = f32[16,3584]{1,0:T(8,128)S(1)} fusion(bf16[3584,4096]{1,0:T(8,128)(2,1)} %get-tuple-element.569, bf16[1,16,4096]{2,0,1:T(2,128)(2,1)S(1)} %constant_dynamic-slice_fusion.6), kind=kOutput, calls=%fused_computation.22.clone.1 | convolution fusion | flops 469762048 | bytes 29720576 | tf_op jit(solution)/shard_map/while/body/eval_jaxpr/dot_general | solution.py:38
  522.8 21.8 %fusion.83 = f32[16,4096]{1,0:T(8,128)S(1)} fusion(bf16[3584,4096]{1,0:T(8,128)(2,1)} %get-tuple-element.571, bf16[3584,4096]{1,0:T(8,128)(2,1)} %get-tuple-element.570, f32[16,3584]{1,0:T(8,128)S(1)} %fusion.82, bf16[1,16,4096]{2,0,1:T(2,128)(2,1)S(1)} %constant_dynamic-slice_fusion.6), kind=kOutput, calls=%fused_computation.8.clone.1 | convolution fusion | flops 939868160 | bytes 59342848 | tf_op jit(solution)/shard_map/while/body/eval_jaxpr/dot_general | solution.py:76
  547.7 54.4 %all-reduce.5.cloned.1.call-done = f32[32,4096]{1,0:T(8,128)} async-done(((f32[32,4096]{1,0:T(8,128)}), f32[32,4096]{1,0:T(8,128)}) %all-reduce.5.cloned.1.call-update) | async-done | bytes 524304 | tf_op jit(solution)/shard_map/while
  (196 shorter events, 66.5 us)
Async XLA Ops:
  6.6 114.4 %all-reduce.5.cloned.1.call-start = ((), (), s32[]{:S(2)}) async-start(), calls=%async_computation | async-start | bytes 1048576 | tf_op jit(solution)/shard_map/while
  39.6 23.7 %copy-start.1 = (u32[32]{0:T(128)S(1)}, u32[32]{0:T(128)}, u32[]{:S(2)}) copy-start(u32[32]{0:T(128)} %get-tuple-element.575) | copy-start | bytes 388 | tf_op jit(solution)/shard_map/while
  123.4 5.8 collective-permute-start
  129.2 112.1 %all-reduce.5.cloned.1.call-start = ((), (), s32[]{:S(2)}) async-start(), calls=%async_computation | async-start | bytes 1048576 | tf_op jit(solution)/shard_map/while
  162.0 23.7 %copy-start.1 = (u32[32]{0:T(128)S(1)}, u32[32]{0:T(128)}, u32[]{:S(2)}) copy-start(u32[32]{0:T(128)} %get-tuple-element.575) | copy-start | bytes 388 | tf_op jit(solution)/shard_map/while
  243.7 5.8 collective-permute-start
  249.5 112.1 %all-reduce.5.cloned.1.call-start = ((), (), s32[]{:S(2)}) async-start(), calls=%async_computation | async-start | bytes 1048576 | tf_op jit(solution)/shard_map/while
  282.3 23.7 %copy-start.1 = (u32[32]{0:T(128)S(1)}, u32[32]{0:T(128)}, u32[]{:S(2)}) copy-start(u32[32]{0:T(128)} %get-tuple-element.575) | copy-start | bytes 388 | tf_op jit(solution)/shard_map/while
  364.0 5.8 collective-permute-start
  369.8 112.1 %all-reduce.5.cloned.1.call-start = ((), (), s32[]{:S(2)}) async-start(), calls=%async_computation | async-start | bytes 1048576 | tf_op jit(solution)/shard_map/while
  402.5 23.7 %copy-start.1 = (u32[32]{0:T(128)S(1)}, u32[32]{0:T(128)}, u32[]{:S(2)}) copy-start(u32[32]{0:T(128)} %get-tuple-element.575) | copy-start | bytes 388 | tf_op jit(solution)/shard_map/while
  484.3 5.8 collective-permute-start
  490.1 112.1 %all-reduce.5.cloned.1.call-start = ((), (), s32[]{:S(2)}) async-start(), calls=%async_computation | async-start | bytes 1048576 | tf_op jit(solution)/shard_map/while
  522.8 23.7 %copy-start.1 = (u32[32]{0:T(128)S(1)}, u32[32]{0:T(128)}, u32[]{:S(2)}) copy-start(u32[32]{0:T(128)} %get-tuple-element.575) | copy-start | bytes 388 | tf_op jit(solution)/shard_map/while
  604.6 5.8 collective-permute-start
  610.4 0.6 copy-start
Sparse Core Ops, SparseCore 0:
  63.5 57.5 all-reduce.4
  185.8 55.4 all-reduce.4
  306.1 55.4 all-reduce.4
  426.4 55.4 all-reduce.4
  546.7 55.4 all-reduce.4
where the time goes:
time: 620 us; the launch traced here: 618 us
  waiting for transfers between devices  297 us (48%)
  matrix products  194 us (31%)
  blocking collectives  71.2 us (11%)
  other arithmetic  17.4 us (3%)
  local copies, waits for them, and re-layouts  15 us (2%)
  between operations  13.1 us (2%)
  starting transfers between devices  6.51 us (1%)
    while x10, waiting for transfers between devices  274 us
    dot_general x5, matrix products, layer(): product = jnp.dot(hidden, w_down, preferred_element_type=jnp.float32)  109 us
    all_gather x5, blocking collectives, layer(): hidden = own_expert(lax.all_gather(mine, 'tensor', axis=1, tiled=True))  71.2 us
    dot_general x5, matrix products, project_rows(): lax.dot_general(rows, weight_rows, (((1,), (1,)), ((), ())), preferred_el...  66.2 us
    ppermute x5, waiting for transfers between devices, from_behind(): return lax.ppermute(block, axis, route)  22.5 us
  transfers between devices with their start and end apart: 10, of which 10 were waited for; matrix products, arithmetic and copies ran while one was open for 0% of the time, Pallas kernels for 0%

commit v1 on v0

v1 whole, which is shorter than its diff:
```python
import functools

import jax
import jax.numpy as jnp
from jax import lax
from jax.experimental import pallas as pl
from jax.experimental.pallas import tpu as pltpu
from jax.sharding import PartitionSpec as P

EPSILON = 1e-05


def normalize(wide, gain):
    scale = lax.rsqrt(jnp.mean(wide * wide, axis=-1, keepdims=True) + EPSILON)
    return (wide * scale * gain).astype(jnp.bfloat16)


def same_block(shape, count):
    rows = lax.broadcasted_iota(jnp.int32, shape, 0)
    columns = lax.broadcasted_iota(jnp.int32, shape, 1)
    return rows, columns, rows // count == columns // count


def pick_rows(ids_across, ids_down, expert, count, slot_count):
    tokens = ids_across.shape[1]
    slots = tokens // count * slot_count
    flag_across = (ids_across[0:1] == expert) | (ids_across[1:2] == expert)
    flag_down = (ids_down[:, 0:1] == expert) | (ids_down[:, 1:2] == expert)
    rows, columns, same = same_block((tokens, tokens), count)
    earlier = same & (rows < columns) & flag_down
    place = jnp.sum(earlier.astype(jnp.int32), axis=0, keepdims=True)
    slot = lax.broadcasted_iota(jnp.int32, (slots, tokens), 0)
    token = lax.broadcasted_iota(jnp.int32, (slots, tokens), 1)
    return flag_across & (slot // slot_count == token // count) & (slot % slot_count == place)


def place_rows(ids_across, ids_down, expert, count, slot_count):
    tokens = ids_across.shape[1]
    slots = tokens // count * slot_count
    flag_across = (ids_across[0:1] == expert) | (ids_across[1:2] == expert)
    flag_down = (ids_down[:, 0:1] == expert) | (ids_down[:, 1:2] == expert)
    rows, columns, same = same_block((tokens, tokens), count)
    earlier = same & (columns < rows) & flag_across
    place = jnp.sum(earlier.astype(jnp.int32), axis=1, keepdims=True)
    token = lax.broadcasted_iota(jnp.int32, (tokens, slots), 0)
    slot = lax.broadcasted_iota(jnp.int32, (tokens, slots), 1)
    return flag_down & (slot // slot_count == token // count) & (slot % slot_count == place)


def mixing_weight(logits, ids_down, expert):
    routed = (ids_down[:, 0:1] == expert) | (ids_down[:, 1:2] == expert)
    partner = jnp.where(ids_down[:, 0:1] == expert, ids_down[:, 1:2], ids_down[:, 0:1])
    columns = lax.broadcasted_iota(jnp.int32, logits.shape, 1)
    other = jnp.sum(jnp.where(columns == partner, logits, 0.0), axis=1, keepdims=True)
    value = 1.0 / (1.0 + jnp.exp(other - logits[:, expert : expert + 1]))
    return jnp.where(routed, value, 0.0)


def pack_kernel(count, slot_count, hidden_ref, gain_ref, across_ref, down_ref, pack_ref):
    normed = normalize(hidden_ref[...].astype(jnp.float32), gain_ref[...])
    half = pack_ref.shape[0] // 2
    for expert in range(2):
        pick = pick_rows(across_ref[...], down_ref[...], expert, count, slot_count)
        rows = jnp.dot(pick.astype(jnp.bfloat16), normed, preferred_element_type=jnp.float32)
        rows = rows.astype(jnp.bfloat16)
        for device in range(half):
            pack_ref[expert * half + device] = rows


def expert_kernel(
    steps, count, slot_count,
    active_ref, x_ref, hidden_ref, gain_ref, router_ref, across_ref, down_ref,
    gate_ref, up_ref, out_ref_w, part_ref, spread_ref, sum_ref,
):
    step = pl.program_id(0)

    @pl.when((step == 0) & (active_ref[0] == 1))
    def _():
        normed = normalize(hidden_ref[...].astype(jnp.float32), gain_ref[...])
        logits = lax.dot_general(
            normed, router_ref[...], (((1,), (1,)), ((), ())), preferred_element_type=jnp.float32
        )
        ids_across = across_ref[...]
        ids_down = down_ref[...]
        for expert in range(2):
            weight = mixing_weight(logits, ids_down, expert)
            place = place_rows(ids_across, ids_down, expert, count, slot_count)
            spread_ref[expert] = jnp.where(place, weight, 0.0)

    @pl.when(active_ref[0] == 1)
    def _():
        x = x_ref[...].reshape(sum_ref.shape)
        contract = (((1,), (1,)), ((), ()))
        gate = lax.dot_general(x, gate_ref[...], contract, preferred_element_type=jnp.float32)
        upward = lax.dot_general(x, up_ref[...], contract, preferred_element_type=jnp.float32)
        hidden = (jax.nn.silu(gate) * upward).astype(jnp.bfloat16)
        product = jnp.dot(hidden, out_ref_w[...], preferred_element_type=jnp.float32)

        @pl.when(step == 0)
        def _():
            sum_ref[...] = product

        @pl.when(step > 0)
        def _():
            sum_ref[...] += product

    @pl.when((step == steps - 1) & (active_ref[0] == 1))
    def _():
        part_ref[...] = sum_ref[...].reshape(part_ref.shape).astype(jnp.bfloat16)


def run_experts(active, x, hidden, gain, router, across, down, w_gate, w_up, w_down, count, slot_count):
    devices, slots, width = x.shape
    units = w_gate.shape[0]
    tile = max(c for c in (256, 128, 64, 32, 16) if units % c == 0)
    steps = units // tile
    tokens = hidden.shape[0]
    moving = lambda i, a: (i * a[0], 0)
    full = lambda array: pl.BlockSpec(array.shape, lambda i, a: (0,) * array.ndim)
    return pl.pallas_call(
        functools.partial(expert_kernel, steps, count, slot_count),
        grid_spec=pltpu.PrefetchScalarGridSpec(
            num_scalar_prefetch=1,
            grid=(steps,),
            in_specs=[full(x), full(hidden), full(gain), full(router), full(across), full(down)]
            + [pl.BlockSpec((tile, width), moving)] * 3,
            out_specs=[
                pl.BlockSpec(x.shape, lambda i, a: (0, 0, 0)),
                pl.BlockSpec((2, tokens, slots), lambda i, a: (0, 0, 0)),
            ],
            scratch_shapes=[pltpu.VMEM((devices * slots, width), jnp.float32)],
        ),
        out_shape=[
            jax.ShapeDtypeStruct(x.shape, jnp.bfloat16),
            jax.ShapeDtypeStruct((2, tokens, slots), jnp.float32),
        ],
        compiler_params=pltpu.CompilerParams(vmem_limit_bytes=40 * 1024 * 1024),
    )(active, x, hidden, gain, router, across, down, w_gate, w_up, w_down)


def combine_kernel(devices, parts_ref, spread_ref, hidden_ref, result_ref):
    total = hidden_ref[...].astype(jnp.float32)
    slots = spread_ref.shape[2]
    half = devices // 2
    for expert in range(2):
        summed = parts_ref[expert * half].astype(jnp.float32)
        for device in range(1, half):
            summed = summed + parts_ref[expert * half + device].astype(jnp.float32)
        spread = spread_ref[expert]
        for slot in range(slots):
            total = total + spread[:, slot : slot + 1] * summed[slot : slot + 1]
    result_ref[...] = total.astype(jnp.bfloat16)


def body(tokens, expert_ids, router_weight, norm_gain, gate_weight, up_weight, down_weight):
    sections = lax.axis_size("section")
    devices = lax.axis_size("tensor")
    section = lax.axis_index("section")
    micro, count, width = tokens.shape
    slot_count = count // 2
    slots = micro * slot_count
    rows = micro * count
    router = jnp.swapaxes(router_weight[0], 0, 1)
    ids_down = expert_ids[0].reshape(rows, 2)
    ids_across = jnp.swapaxes(ids_down, 0, 1)

    def exchange(blocks):
        return lax.all_to_all(blocks, "tensor", 0, 0, tiled=True)

    pack = pl.pallas_call(
        functools.partial(pack_kernel, count, slot_count),
        out_shape=jax.ShapeDtypeStruct((devices, slots, width), jnp.bfloat16),
    )
    combine = pl.pallas_call(
        functools.partial(combine_kernel, devices),
        out_shape=jax.ShapeDtypeStruct((rows, width), jnp.bfloat16),
    )
    hidden = tokens.reshape(rows, width)
    output = hidden
    for layer in range(sections):
        if layer > 0:
            hidden = lax.ppermute(output, "section", [(layer - 1, layer)])
        x = exchange(pack(hidden, norm_gain, ids_across, ids_down))
        active = (section == layer).astype(jnp.int32).reshape(1)
        partial, spread = run_experts(
            active, x, hidden, norm_gain, router, ids_across, ids_down,
            gate_weight[0], up_weight[0], down_weight[0], count, slot_count,
        )
        result = combine(exchange(partial), spread, hidden)
        output = result if layer == 0 else jnp.where(section == layer, result, output)
    return output.reshape(1, micro, count, width)


def solution(mesh):
    return jax.shard_map(
        body,
        mesh=mesh,
        in_specs=(
            P(None, "tensor", None),
            P("section", None, "tensor", None),
            P("section", None, None),
            P("section", None),
            P("section", "tensor", None),
            P("section", "tensor", None),
            P("section", "tensor", None),
        ),
        out_specs=P("section", None, "tensor", None),
        check_vma=False,
    )
```

time: 620 us -> 294 us (0.47)
  matrix products: 194 us -> 0 us
  waiting for transfers between devices: 297 us -> 151 us
  Pallas kernels: 0 us -> 59.8 us
  blocking collectives: 71.2 us -> 51.1 us
  other arithmetic: 17.4 us -> 0.87 us
  between operations: 13.1 us -> 0.2 us
  starting transfers between devices: 6.51 us -> 17.7 us
    while x10 -> x0, waiting for transfers between devices: 274 us -> none
    dot_general x30 -> x0, matrix products: 194 us -> none  [the longest x5 109 us: layer(): product = jnp.dot(hidden, w_down, preferred_element_type=jnp.float32)]
    ppermute x5 -> x3, waiting for transfers between devices: 22.5 us -> 112 us  [body(): hidden = lax.ppermute(output, 'section', [(layer - 1, layer)])]
    all_gather x5 -> x0, blocking collectives: 71.2 us -> none  [layer(): hidden = own_expert(lax.all_gather(mine, 'tensor', axis=1, tiled=True))]
    pallas_call x0 -> x12, Pallas kernels: none -> 59.8 us  [the longest x4 44.8 us: run_experts(): pl.pallas_call(functools.partial(expert_kernel, steps, count, slot_count)...]
    all_to_all x0 -> x4, blocking collectives: none -> 51.1 us  [exchange(): return lax.all_to_all(blocks, 'tensor', 0, 0, tiled=True)]
    all_to_all x0 -> x4, waiting for transfers between devices: none -> 38.6 us  [exchange(): return lax.all_to_all(blocks, 'tensor', 0, 0, tiled=True)]
    all_to_all x0 -> x4, starting transfers between devices: none -> 15.1 us  [exchange(): return lax.all_to_all(blocks, 'tensor', 0, 0, tiled=True)]
  transfers between devices with their start and end apart: 10 -> 7, of which waited for: 10 -> 5; matrix products, arithmetic and copies ran while one was open for 0% -> 0% of each run, Pallas kernels for 0% -> 0%
where the time goes in v1:
time: 294 us; the launch traced here: 292 us
  waiting for transfers between devices  151 us (51%)
  Pallas kernels  59.8 us (20%)
  blocking collectives  51.1 us (17%)
  starting transfers between devices  17.7 us (6%)
  local copies, waits for them, and re-layouts  11.8 us (4%)
    ppermute x3, waiting for transfers between devices, body(): hidden = lax.ppermute(output, 'section', [(layer - 1, layer)])  112 us
    all_to_all x4, blocking collectives, exchange(): return lax.all_to_all(blocks, 'tensor', 0, 0, tiled=True)  51.1 us
    pallas_call x4, Pallas kernels, run_experts(): pl.pallas_call(functools.partial(expert_kernel, steps, count, slot_count)...  44.8 us
    all_to_all x4, waiting for transfers between devices, exchange(): return lax.all_to_all(blocks, 'tensor', 0, 0, tiled=True)  38.6 us
    all_to_all x4, starting transfers between devices, exchange(): return lax.all_to_all(blocks, 'tensor', 0, 0, tiled=True)  15.1 us
    unnamed x55, local copies, waits for them, and re-layouts  8.86 us
    pallas_call x4, Pallas kernels, body(): x = exchange(pack(hidden, norm_gain, ids_across, ids_down))  7.66 us
    pallas_call x4, Pallas kernels, body(): result = combine(exchange(partial), spread, hidden)  7.26 us
  transfers between devices with their start and end apart: 7, of which 5 were waited for; matrix products, arithmetic and copies ran while one was open for 0% of the time, Pallas kernels for 0%

profile of v1, /device:TPU:6, one launch (start us, length us, event | category | flops | bytes accessed | tf_op | source)
XLA Modules:
  0.0 292.2 jit_solution(9760808251695551020)
XLA Ops:
  2.9 1.9 shard_map.73
  4.8 4.9 %all-to-all-start = ((bf16[8,4,4096]{2,1,0:T(4,128)(2,1)}), bf16[8,4,4096]{2,1,0:T(4,128)(2,1)S(1)}, u32[]{:S(2)}, u32[]{:S(2)}) async-start(bf16[8,4,4096]{2,1,0:T(4,128)(2,1)} %shard_map.73), calls=%async_computation | async-start | bytes 524288 | tf_op jit(solution)/shard_map/all_to_all | solution.py:168
  9.7 9.7 %all-to-all-done.x_ref = bf16[8,4,4096]{2,1,0:T(4,128)(2,1)S(1)} async-done(((bf16[8,4,4096]{2,1,0:T(4,128)(2,1)}), bf16[8,4,4096]{2,1,0:T(4,128)(2,1)S(1)}, u32[]{:S(2)}, u32[]{:S(2)}) %all-to-all-start) | async-done | bytes 262176 | tf_op jit(solution)/shard_map/all_to_all | solution.py:168
  23.2 2.9 shard_map.74
  26.1 12.8 %all_to_all.40.parts_ref = bf16[8,4,4096]{2,1,0:T(4,128)(2,1)} all-to-all(bf16[8,4,4096]{2,1,0:T(4,128)(2,1)S(1)} %get-tuple-element.13), channel_id=1, replica_groups=mesh['section'=4,'tensor'=8] {'tensor'}, dimensions={0} | all-to-all | bytes 524288 | tf_op jit(solution)/shard_map/all_to_all | solution.py:168
  38.9 1.8 shard_map.75
  42.0 1.9 shard_map.76
  43.9 3.4 %all-to-all-start.2 = ((bf16[8,4,4096]{2,1,0:T(4,128)(2,1)}), bf16[8,4,4096]{2,1,0:T(4,128)(2,1)S(1)}, u32[]{:S(2)}, u32[]{:S(2)}) async-start(bf16[8,4,4096]{2,1,0:T(4,128)(2,1)} %shard_map.76), calls=%async_computation.2 | async-start | bytes 524288 | tf_op jit(solution)/shard_map/all_to_all | solution.py:168
  47.3 9.6 %all-to-all-done.2.x_ref = bf16[8,4,4096]{2,1,0:T(4,128)(2,1)S(1)} async-done(((bf16[8,4,4096]{2,1,0:T(4,128)(2,1)}), bf16[8,4,4096]{2,1,0:T(4,128)(2,1)S(1)}, u32[]{:S(2)}, u32[]{:S(2)}) %all-to-all-start.2) | async-done | bytes 262176 | tf_op jit(solution)/shard_map/all_to_all | solution.py:168
  57.8 2.9 shard_map.77
  60.7 12.8 %all_to_all.41.parts_ref = bf16[8,4,4096]{2,1,0:T(4,128)(2,1)} all-to-all(bf16[8,4,4096]{2,1,0:T(4,128)(2,1)S(1)} %get-tuple-element.15), channel_id=1, replica_groups=mesh['section'=4,'tensor'=8] {'tensor'}, dimensions={0} | all-to-all | bytes 524288 | tf_op jit(solution)/shard_map/all_to_all | solution.py:168
  76.6 1.9 shard_map.79
  78.6 3.4 %all-to-all-start.4 = ((bf16[8,4,4096]{2,1,0:T(4,128)(2,1)}), bf16[8,4,4096]{2,1,0:T(4,128)(2,1)S(1)}, u32[]{:S(2)}, u32[]{:S(2)}) async-start(bf16[8,4,4096]{2,1,0:T(4,128)(2,1)} %shard_map.79), calls=%async_computation.4 | async-start | bytes 524288 | tf_op jit(solution)/shard_map/all_to_all | solution.py:168
  82.0 9.6 %all-to-all-done.4.x_ref = bf16[8,4,4096]{2,1,0:T(4,128)(2,1)S(1)} async-done(((bf16[8,4,4096]{2,1,0:T(4,128)(2,1)}), bf16[8,4,4096]{2,1,0:T(4,128)(2,1)S(1)}, u32[]{:S(2)}, u32[]{:S(2)}) %all-to-all-start.4) | async-done | bytes 262176 | tf_op jit(solution)/shard_map/all_to_all | solution.py:168
  92.5 2.9 shard_map.80
  95.3 12.8 %all_to_all.42.parts_ref = bf16[8,4,4096]{2,1,0:T(4,128)(2,1)} all-to-all(bf16[8,4,4096]{2,1,0:T(4,128)(2,1)S(1)} %get-tuple-element.17), channel_id=1, replica_groups=mesh['section'=4,'tensor'=8] {'tensor'}, dimensions={0} | all-to-all | bytes 524288 | tf_op jit(solution)/shard_map/all_to_all | solution.py:168
  108.1 1.8 shard_map.81
  111.3 112.2 %collective-permute-done.2.hidden_ref = bf16[8,4096]{1,0:T(8,128)(2,1)S(1)} collective-permute-done((bf16[8,4096]{1,0:T(8,128)(2,1)S(1)}, bf16[8,4096]{1,0:T(8,128)(2,1)S(1)}, u32[]{:S(2)}, u32[]{:S(2)}) %collective-permute-start.2) | collective-permute-done | bytes 65568 | tf_op jit(solution)/shard_map/ppermute | solution.py:182
  224.1 1.9 shard_map.82
  226.0 3.4 %all-to-all-start.6 = ((bf16[8,4,4096]{2,1,0:T(4,128)(2,1)}), bf16[8,4,4096]{2,1,0:T(4,128)(2,1)S(1)}, u32[]{:S(2)}, u32[]{:S(2)}) async-start(bf16[8,4,4096]{2,1,0:T(4,128)(2,1)} %shard_map.82), calls=%async_computation.6 | async-start | bytes 524288 | tf_op jit(solution)/shard_map/all_to_all | solution.py:168
  229.5 9.6 %all-to-all-done.6.x_ref = bf16[8,4,4096]{2,1,0:T(4,128)(2,1)S(1)} async-done(((bf16[8,4,4096]{2,1,0:T(4,128)(2,1)}), bf16[8,4,4096]{2,1,0:T(4,128)(2,1)S(1)}, u32[]{:S(2)}, u32[]{:S(2)}) %all-to-all-start.6) | async-done | bytes 262176 | tf_op jit(solution)/shard_map/all_to_all | solution.py:168
  239.9 36.2 %shard_map.83 = (bf16[8,4,4096]{2,1,0:T(4,128)(2,1)S(1)}, f32[2,8,4]{2,1,0:T(8,128)S(1)}) custom-call(s32[1]{0:T(128)} %bitcast.active_ref, bf16[8,4,4096]{2,1,0:T(4,128)(2,1)S(1)} %all-to-all-done.6.x_ref, bf16[8,4096]{1,0:T(8,128)(2,1)S(1)} %copy-done.8, f32[1,4096]{1,0:T(1,128)S(1)} %copy-done.5, bf16[8,4096]{1,0:T(8,128)(2,1)S(1)} %bitcast.16, ...), custom_call_target="tpu_custom_call" | custom-call | tf_op jit(solution)/shard_map/pallas_call | solution.py:120
  276.1 12.8 %all_to_all.43.parts_ref = bf16[8,4,4096]{2,1,0:T(4,128)(2,1)} all-to-all(bf16[8,4,4096]{2,1,0:T(4,128)(2,1)S(1)} %get-tuple-element.19), channel_id=1, replica_groups=mesh['section'=4,'tensor'=8] {'tensor'}, dimensions={0} | all-to-all | bytes 524288 | tf_op jit(solution)/shard_map/all_to_all | solution.py:168
  288.9 1.8 shard_map.84
  (68 shorter events, 17.1 us)
Async XLA Ops:
  0.8 2.2 copy-start.17
  4.8 14.6 %all-to-all-start = ((bf16[8,4,4096]{2,1,0:T(4,128)(2,1)}), bf16[8,4,4096]{2,1,0:T(4,128)(2,1)S(1)}, u32[]{:S(2)}, u32[]{:S(2)}) async-start(bf16[8,4,4096]{2,1,0:T(4,128)(2,1)} %shard_map.73), calls=%async_computation | async-start | bytes 524288 | tf_op jit(solution)/shard_map/all_to_all | solution.py:168
  23.2 33.8 %copy-start.1 = (bf16[1,4096,8]{1,2,0:T(8,128)(2,1)S(1)}, bf16[1,4096,8]{1,2,0:T(8,128)(2,1)}, u32[]{:S(2)}) copy-start(bf16[1,4096,8]{1,2,0:T(8,128)(2,1)} %param.9) | copy-start | bytes 196612
  23.2 33.8 %copy-start.3 = (f32[1,4096]{1,0:T(1,128)S(1)}, f32[1,4096]{1,0:T(1,128)}, u32[]{:S(2)}) copy-start(f32[1,4096]{1,0:T(1,128)} %gain_ref.15) | copy-start | bytes 49156
  23.2 33.8 %copy-start.14 = (s32[8,2]{1,0:T(8,128)S(1)}, s32[8,2]{1,0:T(8,128)}, u32[]{:S(2)}) copy-start(s32[8,2]{1,0:T(8,128)} %copy.9.down_ref) | copy-start | bytes 196
  23.2 33.8 %copy-start.19 = (s32[8,2]{0,1:T(2,128)S(1)}, s32[8,2]{0,1:T(2,128)}, u32[]{:S(2)}) copy-start(s32[8,2]{0,1:T(2,128)} %copy-done.17) | copy-start | bytes 196
  26.1 12.8 %copy-start.23 = (f32[2,8,4]{2,1,0:T(8,128)}, f32[2,8,4]{2,1,0:T(8,128)S(1)}, u32[]{:S(2)}) copy-start(f32[2,8,4]{2,1,0:T(8,128)S(1)} %get-tuple-element.14.spread_ref) | copy-start | bytes 772
  40.7 0.7 collective-permute-start
  43.9 13.1 %all-to-all-start.2 = ((bf16[8,4,4096]{2,1,0:T(4,128)(2,1)}), bf16[8,4,4096]{2,1,0:T(4,128)(2,1)S(1)}, u32[]{:S(2)}, u32[]{:S(2)}) async-start(bf16[8,4,4096]{2,1,0:T(4,128)(2,1)} %shard_map.76), calls=%async_computation.2 | async-start | bytes 524288 | tf_op jit(solution)/shard_map/all_to_all | solution.py:168
  57.0 0.8 copy-start.10
  57.8 17.5 %copy-start.26 = (bf16[8,4096]{1,0:T(8,128)(2,1)S(1)}, bf16[8,4096]{1,0:T(8,128)(2,1)}, u32[]{:S(2)}) copy-start(bf16[8,4096]{1,0:T(8,128)(2,1)} %shard_map.75) | copy-start | bytes 196612
  57.8 33.8 %copy-start.4 = (f32[1,4096]{1,0:T(1,128)S(1)}, f32[1,4096]{1,0:T(1,128)}, u32[]{:S(2)}) copy-start(f32[1,4096]{1,0:T(1,128)} %gain_ref.15) | copy-start | bytes 49156
  57.8 33.8 %copy-start.15 = (s32[8,2]{1,0:T(8,128)S(1)}, s32[8,2]{1,0:T(8,128)}, u32[]{:S(2)}) copy-start(s32[8,2]{1,0:T(8,128)} %copy.9.down_ref) | copy-start | bytes 196
  57.8 33.8 %copy-start.20 = (s32[8,2]{0,1:T(2,128)S(1)}, s32[8,2]{0,1:T(2,128)}, u32[]{:S(2)}) copy-start(s32[8,2]{0,1:T(2,128)} %copy-done.17) | copy-start | bytes 196
  60.7 12.8 %copy-start.24 = (f32[2,8,4]{2,1,0:T(8,128)}, f32[2,8,4]{2,1,0:T(8,128)S(1)}, u32[]{:S(2)}) copy-start(f32[2,8,4]{2,1,0:T(8,128)S(1)} %get-tuple-element.16.spread_ref) | copy-start | bytes 772
  75.3 0.7 collective-permute-start.1
  78.6 13.1 %all-to-all-start.4 = ((bf16[8,4,4096]{2,1,0:T(4,128)(2,1)}), bf16[8,4,4096]{2,1,0:T(4,128)(2,1)S(1)}, u32[]{:S(2)}, u32[]{:S(2)}) async-start(bf16[8,4,4096]{2,1,0:T(4,128)(2,1)} %shard_map.79), calls=%async_computation.4 | async-start | bytes 524288 | tf_op jit(solution)/shard_map/all_to_all | solution.py:168
  92.5 146.6 %copy-start.5 = (f32[1,4096]{1,0:T(1,128)S(1)}, f32[1,4096]{1,0:T(1,128)}, u32[]{:S(2)}) copy-start(f32[1,4096]{1,0:T(1,128)} %gain_ref.15) | copy-start | bytes 49156
  92.5 146.6 %copy-start.16 = (s32[8,2]{1,0:T(8,128)S(1)}, s32[8,2]{1,0:T(8,128)}, u32[]{:S(2)}) copy-start(s32[8,2]{1,0:T(8,128)} %copy.9.down_ref) | copy-start | bytes 196
  92.5 146.6 %copy-start.21 = (s32[8,2]{0,1:T(2,128)S(1)}, s32[8,2]{0,1:T(2,128)}, u32[]{:S(2)}) copy-start(s32[8,2]{0,1:T(2,128)} %copy-done.17) | copy-start | bytes 196
  95.3 12.8 %copy-start.25 = (f32[2,8,4]{2,1,0:T(8,128)}, f32[2,8,4]{2,1,0:T(8,128)S(1)}, u32[]{:S(2)}) copy-start(f32[2,8,4]{2,1,0:T(8,128)S(1)} %get-tuple-element.18.spread_ref) | copy-start | bytes 772
  110.0 113.5 %collective-permute-start.2 = (bf16[8,4096]{1,0:T(8,128)(2,1)S(1)}, bf16[8,4096]{1,0:T(8,128)(2,1)S(1)}, u32[]{:S(2)}, u32[]{:S(2)}) collective-permute-start(bf16[8,4096]{1,0:T(8,128)(2,1)S(1)} %broadcast_select_fusion.1), channel_id=1, source_target_pairs={{16,24},{17,25},{18,26},{19,27},{20,28},{21,29},{22,30},{23,31}} | collective-permute-start | bytes 196616 | tf_op jit(solution)/shard_map/ppermute | solution.py:182
  226.0 13.1 %all-to-all-start.6 = ((bf16[8,4,4096]{2,1,0:T(4,128)(2,1)}), bf16[8,4,4096]{2,1,0:T(4,128)(2,1)S(1)}, u32[]{:S(2)}, u32[]{:S(2)}) async-start(bf16[8,4,4096]{2,1,0:T(4,128)(2,1)} %shard_map.82), calls=%async_computation.6 | async-start | bytes 524288 | tf_op jit(solution)/shard_map/all_to_all | solution.py:168
  276.1 12.8 %copy-start.22 = (f32[2,8,4]{2,1,0:T(8,128)}, f32[2,8,4]{2,1,0:T(8,128)S(1)}, u32[]{:S(2)}) copy-start(f32[2,8,4]{2,1,0:T(8,128)S(1)} %get-tuple-element.20.spread_ref) | copy-start | bytes 772
  (10 other events, 7.3 us)

commit v2 on v1

--- a/solution.py
+++ b/solution.py
@@ -112,7 +112,7 @@
 def run_experts(active, x, hidden, gain, router, across, down, w_gate, w_up, w_down, count, slot_count):
     devices, slots, width = x.shape
     units = w_gate.shape[0]
-    tile = max(c for c in (256, 128, 64, 32, 16) if units % c == 0)
+    tile = max(c for c in (512, 256, 128, 64, 32, 16) if units % c == 0)
     steps = units // tile
     tokens = hidden.shape[0]
     moving = lambda i, a: (i * a[0], 0)

time: 294 us -> 281 us (0.956)
  waiting for transfers between devices: 151 us -> 136 us
    ppermute x3, waiting for transfers between devices: 112 us -> 97.3 us  [body(): hidden = lax.ppermute(output, 'section', [(layer - 1, layer)])]
where the time goes in v2:
time: 281 us; the launch traced here: 280 us
  waiting for transfers between devices  136 us (48%)
  Pallas kernels  62 us (22%)
  blocking collectives  51.1 us (18%)
  starting transfers between devices  17.9 us (6%)
  local copies, waits for them, and re-layouts  11.8 us (4%)
    ppermute x3, waiting for transfers between devices, body(): hidden = lax.ppermute(output, 'section', [(layer - 1, layer)])  97.3 us
    all_to_all x4, blocking collectives, exchange(): return lax.all_to_all(blocks, 'tensor', 0, 0, tiled=True)  51.1 us
    pallas_call x4, Pallas kernels, run_experts(): pl.pallas_call(functools.partial(expert_kernel, steps, count, slot_count)...  47.1 us
    all_to_all x4, waiting for transfers between devices, exchange(): return lax.all_to_all(blocks, 'tensor', 0, 0, tiled=True)  38.4 us
    all_to_all x4, starting transfers between devices, exchange(): return lax.all_to_all(blocks, 'tensor', 0, 0, tiled=True)  15.3 us
    unnamed x55, local copies, waits for them, and re-layouts  8.86 us
    pallas_call x4, Pallas kernels, body(): x = exchange(pack(hidden, norm_gain, ids_across, ids_down))  7.65 us
    pallas_call x4, Pallas kernels, body(): result = combine(exchange(partial), spread, hidden)  7.26 us
  transfers between devices with their start and end apart: 7, of which 5 were waited for; matrix products, arithmetic and copies ran while one was open for 0% of the time, Pallas kernels for 0%

profile of v2, /device:TPU:6, one launch (start us, length us, event | category | flops | bytes accessed | tf_op | source)
XLA Modules:
  0.0 279.5 jit_solution(18198560716971798441)
XLA Ops:
  2.9 1.9 shard_map.73
  4.9 4.9 %all-to-all-start = ((bf16[8,4,4096]{2,1,0:T(4,128)(2,1)}), bf16[8,4,4096]{2,1,0:T(4,128)(2,1)S(1)}, u32[]{:S(2)}, u32[]{:S(2)}) async-start(bf16[8,4,4096]{2,1,0:T(4,128)(2,1)} %shard_map.73), calls=%async_computation | async-start | bytes 524288 | tf_op jit(solution)/shard_map/all_to_all | solution.py:168
  9.7 9.7 %all-to-all-done.x_ref = bf16[8,4,4096]{2,1,0:T(4,128)(2,1)S(1)} async-done(((bf16[8,4,4096]{2,1,0:T(4,128)(2,1)}), bf16[8,4,4096]{2,1,0:T(4,128)(2,1)S(1)}, u32[]{:S(2)}, u32[]{:S(2)}) %all-to-all-start) | async-done | bytes 262176 | tf_op jit(solution)/shard_map/all_to_all | solution.py:168
  23.2 4.7 %shard_map.74 = (bf16[8,4,4096]{2,1,0:T(4,128)(2,1)S(1)}, f32[2,8,4]{2,1,0:T(8,128)S(1)}) custom-call(s32[1]{0:T(128)} %bitcast.3.active_ref, bf16[8,4,4096]{2,1,0:T(4,128)(2,1)S(1)} %all-to-all-done.x_ref, bf16[8,4096]{1,0:T(8,128)(2,1)S(1)} %copy-done.6, f32[1,4096]{1,0:T(1,128)S(1)} %copy-done.2, bf16[8,4096]{1,0:T(8,128)(2,1)S(1)} %bitcast.13, ...), custom_call_target="tpu_custom_call" | custom-call | tf_op jit(solution)/shard_map/pallas_call | solution.py:120
  27.9 12.8 %all_to_all.40.parts_ref = bf16[8,4,4096]{2,1,0:T(4,128)(2,1)} all-to-all(bf16[8,4,4096]{2,1,0:T(4,128)(2,1)S(1)} %get-tuple-element.13), channel_id=1, replica_groups=mesh['section'=4,'tensor'=8] {'tensor'}, dimensions={0} | all-to-all | bytes 524288 | tf_op jit(solution)/shard_map/all_to_all | solution.py:168
  40.7 1.8 shard_map.75
  43.8 1.9 shard_map.76
  45.7 3.4 %all-to-all-start.2 = ((bf16[8,4,4096]{2,1,0:T(4,128)(2,1)}), bf16[8,4,4096]{2,1,0:T(4,128)(2,1)S(1)}, u32[]{:S(2)}, u32[]{:S(2)}) async-start(bf16[8,4,4096]{2,1,0:T(4,128)(2,1)} %shard_map.76), calls=%async_computation.2 | async-start | bytes 524288 | tf_op jit(solution)/shard_map/all_to_all | solution.py:168
  49.1 9.6 %all-to-all-done.2.x_ref = bf16[8,4,4096]{2,1,0:T(4,128)(2,1)S(1)} async-done(((bf16[8,4,4096]{2,1,0:T(4,128)(2,1)}), bf16[8,4,4096]{2,1,0:T(4,128)(2,1)S(1)}, u32[]{:S(2)}, u32[]{:S(2)}) %all-to-all-start.2) | async-done | bytes 262176 | tf_op jit(solution)/shard_map/all_to_all | solution.py:168
  59.6 4.7 %shard_map.77 = (bf16[8,4,4096]{2,1,0:T(4,128)(2,1)S(1)}, f32[2,8,4]{2,1,0:T(8,128)S(1)}) custom-call(s32[1]{0:T(128)} %bitcast.2.active_ref, bf16[8,4,4096]{2,1,0:T(4,128)(2,1)S(1)} %all-to-all-done.2.x_ref, bf16[8,4096]{1,0:T(8,128)(2,1)S(1)} %copy-done.10, f32[1,4096]{1,0:T(1,128)S(1)} %copy-done.3, bf16[8,4096]{1,0:T(8,128)(2,1)S(1)} %bitcast.14, ...), custom_call_target="tpu_custom_call" | custom-call | tf_op jit(solution)/shard_map/pallas_call | solution.py:120
  64.3 12.8 %all_to_all.41.parts_ref = bf16[8,4,4096]{2,1,0:T(4,128)(2,1)} all-to-all(bf16[8,4,4096]{2,1,0:T(4,128)(2,1)S(1)} %get-tuple-element.15), channel_id=1, replica_groups=mesh['section'=4,'tensor'=8] {'tensor'}, dimensions={0} | all-to-all | bytes 524288 | tf_op jit(solution)/shard_map/all_to_all | solution.py:168
  80.2 1.9 shard_map.79
  82.1 3.4 %all-to-all-start.4 = ((bf16[8,4,4096]{2,1,0:T(4,128)(2,1)}), bf16[8,4,4096]{2,1,0:T(4,128)(2,1)S(1)}, u32[]{:S(2)}, u32[]{:S(2)}) async-start(bf16[8,4,4096]{2,1,0:T(4,128)(2,1)} %shard_map.79), calls=%async_computation.4 | async-start | bytes 524288 | tf_op jit(solution)/shard_map/all_to_all | solution.py:168
  85.6 9.6 %all-to-all-done.4.x_ref = bf16[8,4,4096]{2,1,0:T(4,128)(2,1)S(1)} async-done(((bf16[8,4,4096]{2,1,0:T(4,128)(2,1)}), bf16[8,4,4096]{2,1,0:T(4,128)(2,1)S(1)}, u32[]{:S(2)}, u32[]{:S(2)}) %all-to-all-start.4) | async-done | bytes 262176 | tf_op jit(solution)/shard_map/all_to_all | solution.py:168
  96.1 4.7 %shard_map.80 = (bf16[8,4,4096]{2,1,0:T(4,128)(2,1)S(1)}, f32[2,8,4]{2,1,0:T(8,128)S(1)}) custom-call(s32[1]{0:T(128)} %bitcast.1.active_ref, bf16[8,4,4096]{2,1,0:T(4,128)(2,1)S(1)} %all-to-all-done.4.x_ref, bf16[8,4096]{1,0:T(8,128)(2,1)S(1)} %copy-done.12, f32[1,4096]{1,0:T(1,128)S(1)} %copy-done.4, bf16[8,4096]{1,0:T(8,128)(2,1)S(1)} %bitcast.15, ...), custom_call_target="tpu_custom_call" | custom-call | tf_op jit(solution)/shard_map/pallas_call | solution.py:120
  100.7 12.8 %all_to_all.42.parts_ref = bf16[8,4,4096]{2,1,0:T(4,128)(2,1)} all-to-all(bf16[8,4,4096]{2,1,0:T(4,128)(2,1)S(1)} %get-tuple-element.17), channel_id=1, replica_groups=mesh['section'=4,'tensor'=8] {'tensor'}, dimensions={0} | all-to-all | bytes 524288 | tf_op jit(solution)/shard_map/all_to_all | solution.py:168
  113.5 1.8 shard_map.81
  116.6 97.3 %collective-permute-done.2.hidden_ref = bf16[8,4096]{1,0:T(8,128)(2,1)S(1)} collective-permute-done((bf16[8,4096]{1,0:T(8,128)(2,1)S(1)}, bf16[8,4096]{1,0:T(8,128)(2,1)S(1)}, u32[]{:S(2)}, u32[]{:S(2)}) %collective-permute-start.2) | collective-permute-done | bytes 65568 | tf_op jit(solution)/shard_map/ppermute | solution.py:182
  214.6 1.9 shard_map.82
  216.5 3.6 %all-to-all-start.6 = ((bf16[8,4,4096]{2,1,0:T(4,128)(2,1)}), bf16[8,4,4096]{2,1,0:T(4,128)(2,1)S(1)}, u32[]{:S(2)}, u32[]{:S(2)}) async-start(bf16[8,4,4096]{2,1,0:T(4,128)(2,1)} %shard_map.82), calls=%async_computation.6 | async-start | bytes 524288 | tf_op jit(solution)/shard_map/all_to_all | solution.py:168
  220.1 9.4 %all-to-all-done.6.x_ref = bf16[8,4,4096]{2,1,0:T(4,128)(2,1)S(1)} async-done(((bf16[8,4,4096]{2,1,0:T(4,128)(2,1)}), bf16[8,4,4096]{2,1,0:T(4,128)(2,1)S(1)}, u32[]{:S(2)}, u32[]{:S(2)}) %all-to-all-start.6) | async-done | bytes 262176 | tf_op jit(solution)/shard_map/all_to_all | solution.py:168
  230.4 33.0 %shard_map.83 = (bf16[8,4,4096]{2,1,0:T(4,128)(2,1)S(1)}, f32[2,8,4]{2,1,0:T(8,128)S(1)}) custom-call(s32[1]{0:T(128)} %bitcast.active_ref, bf16[8,4,4096]{2,1,0:T(4,128)(2,1)S(1)} %all-to-all-done.6.x_ref, bf16[8,4096]{1,0:T(8,128)(2,1)S(1)} %copy-done.8, f32[1,4096]{1,0:T(1,128)S(1)} %copy-done.5, bf16[8,4096]{1,0:T(8,128)(2,1)S(1)} %bitcast.16, ...), custom_call_target="tpu_custom_call" | custom-call | tf_op jit(solution)/shard_map/pallas_call | solution.py:120
  263.4 12.8 %all_to_all.43.parts_ref = bf16[8,4,4096]{2,1,0:T(4,128)(2,1)} all-to-all(bf16[8,4,4096]{2,1,0:T(4,128)(2,1)S(1)} %get-tuple-element.19), channel_id=1, replica_groups=mesh['section'=4,'tensor'=8] {'tensor'}, dimensions={0} | all-to-all | bytes 524288 | tf_op jit(solution)/shard_map/all_to_all | solution.py:168
  276.2 1.8 shard_map.84
  (68 shorter events, 17.1 us)
Async XLA Ops:
  0.8 2.2 copy-start.17
  4.9 14.6 %all-to-all-start = ((bf16[8,4,4096]{2,1,0:T(4,128)(2,1)}), bf16[8,4,4096]{2,1,0:T(4,128)(2,1)S(1)}, u32[]{:S(2)}, u32[]{:S(2)}) async-start(bf16[8,4,4096]{2,1,0:T(4,128)(2,1)} %shard_map.73), calls=%async_computation | async-start | bytes 524288 | tf_op jit(solution)/shard_map/all_to_all | solution.py:168
  23.2 35.6 %copy-start.1 = (bf16[1,4096,8]{1,2,0:T(8,128)(2,1)S(1)}, bf16[1,4096,8]{1,2,0:T(8,128)(2,1)}, u32[]{:S(2)}) copy-start(bf16[1,4096,8]{1,2,0:T(8,128)(2,1)} %param.9) | copy-start | bytes 196612
  23.2 35.6 %copy-start.3 = (f32[1,4096]{1,0:T(1,128)S(1)}, f32[1,4096]{1,0:T(1,128)}, u32[]{:S(2)}) copy-start(f32[1,4096]{1,0:T(1,128)} %gain_ref.15) | copy-start | bytes 49156
  23.2 35.6 %copy-start.14 = (s32[8,2]{1,0:T(8,128)S(1)}, s32[8,2]{1,0:T(8,128)}, u32[]{:S(2)}) copy-start(s32[8,2]{1,0:T(8,128)} %copy.9.down_ref) | copy-start | bytes 196
  23.2 35.6 %copy-start.19 = (s32[8,2]{0,1:T(2,128)S(1)}, s32[8,2]{0,1:T(2,128)}, u32[]{:S(2)}) copy-start(s32[8,2]{0,1:T(2,128)} %copy-done.17) | copy-start | bytes 196
  27.9 12.8 %copy-start.23 = (f32[2,8,4]{2,1,0:T(8,128)}, f32[2,8,4]{2,1,0:T(8,128)S(1)}, u32[]{:S(2)}) copy-start(f32[2,8,4]{2,1,0:T(8,128)S(1)} %get-tuple-element.14.spread_ref) | copy-start | bytes 772
  42.5 0.7 collective-permute-start
  45.7 13.1 %all-to-all-start.2 = ((bf16[8,4,4096]{2,1,0:T(4,128)(2,1)}), bf16[8,4,4096]{2,1,0:T(4,128)(2,1)S(1)}, u32[]{:S(2)}, u32[]{:S(2)}) async-start(bf16[8,4,4096]{2,1,0:T(4,128)(2,1)} %shard_map.76), calls=%async_computation.2 | async-start | bytes 524288 | tf_op jit(solution)/shard_map/all_to_all | solution.py:168
  58.8 0.8 copy-start.10
  59.6 19.3 %copy-start.26 = (bf16[8,4096]{1,0:T(8,128)(2,1)S(1)}, bf16[8,4096]{1,0:T(8,128)(2,1)}, u32[]{:S(2)}) copy-start(bf16[8,4096]{1,0:T(8,128)(2,1)} %shard_map.75) | copy-start | bytes 196612
  59.6 35.6 %copy-start.4 = (f32[1,4096]{1,0:T(1,128)S(1)}, f32[1,4096]{1,0:T(1,128)}, u32[]{:S(2)}) copy-start(f32[1,4096]{1,0:T(1,128)} %gain_ref.15) | copy-start | bytes 49156
  59.6 35.6 %copy-start.15 = (s32[8,2]{1,0:T(8,128)S(1)}, s32[8,2]{1,0:T(8,128)}, u32[]{:S(2)}) copy-start(s32[8,2]{1,0:T(8,128)} %copy.9.down_ref) | copy-start | bytes 196
  59.6 35.6 %copy-start.20 = (s32[8,2]{0,1:T(2,128)S(1)}, s32[8,2]{0,1:T(2,128)}, u32[]{:S(2)}) copy-start(s32[8,2]{0,1:T(2,128)} %copy-done.17) | copy-start | bytes 196
  64.3 12.8 %copy-start.24 = (f32[2,8,4]{2,1,0:T(8,128)}, f32[2,8,4]{2,1,0:T(8,128)S(1)}, u32[]{:S(2)}) copy-start(f32[2,8,4]{2,1,0:T(8,128)S(1)} %get-tuple-element.16.spread_ref) | copy-start | bytes 772
  78.9 0.7 collective-permute-start.1
  82.1 13.1 %all-to-all-start.4 = ((bf16[8,4,4096]{2,1,0:T(4,128)(2,1)}), bf16[8,4,4096]{2,1,0:T(4,128)(2,1)S(1)}, u32[]{:S(2)}, u32[]{:S(2)}) async-start(bf16[8,4,4096]{2,1,0:T(4,128)(2,1)} %shard_map.79), calls=%async_computation.4 | async-start | bytes 524288 | tf_op jit(solution)/shard_map/all_to_all | solution.py:168
  96.0 133.5 %copy-start.5 = (f32[1,4096]{1,0:T(1,128)S(1)}, f32[1,4096]{1,0:T(1,128)}, u32[]{:S(2)}) copy-start(f32[1,4096]{1,0:T(1,128)} %gain_ref.15) | copy-start | bytes 49156
  96.1 133.5 %copy-start.16 = (s32[8,2]{1,0:T(8,128)S(1)}, s32[8,2]{1,0:T(8,128)}, u32[]{:S(2)}) copy-start(s32[8,2]{1,0:T(8,128)} %copy.9.down_ref) | copy-start | bytes 196
  96.1 133.5 %copy-start.21 = (s32[8,2]{0,1:T(2,128)S(1)}, s32[8,2]{0,1:T(2,128)}, u32[]{:S(2)}) copy-start(s32[8,2]{0,1:T(2,128)} %copy-done.17) | copy-start | bytes 196
  100.7 12.8 %copy-start.25 = (f32[2,8,4]{2,1,0:T(8,128)}, f32[2,8,4]{2,1,0:T(8,128)S(1)}, u32[]{:S(2)}) copy-start(f32[2,8,4]{2,1,0:T(8,128)S(1)} %get-tuple-element.18.spread_ref) | copy-start | bytes 772
  115.3 98.6 %collective-permute-start.2 = (bf16[8,4096]{1,0:T(8,128)(2,1)S(1)}, bf16[8,4096]{1,0:T(8,128)(2,1)S(1)}, u32[]{:S(2)}, u32[]{:S(2)}) collective-permute-start(bf16[8,4096]{1,0:T(8,128)(2,1)S(1)} %broadcast_select_fusion.1), channel_id=1, source_target_pairs={{16,24},{17,25},{18,26},{19,27},{20,28},{21,29},{22,30},{23,31}} | collective-permute-start | bytes 196616 | tf_op jit(solution)/shard_map/ppermute | solution.py:182
  216.5 13.1 %all-to-all-start.6 = ((bf16[8,4,4096]{2,1,0:T(4,128)(2,1)}), bf16[8,4,4096]{2,1,0:T(4,128)(2,1)S(1)}, u32[]{:S(2)}, u32[]{:S(2)}) async-start(bf16[8,4,4096]{2,1,0:T(4,128)(2,1)} %shard_map.82), calls=%async_computation.6 | async-start | bytes 524288 | tf_op jit(solution)/shard_map/all_to_all | solution.py:168
  263.4 12.8 %copy-start.22 = (f32[2,8,4]{2,1,0:T(8,128)}, f32[2,8,4]{2,1,0:T(8,128)S(1)}, u32[]{:S(2)}) copy-start(f32[2,8,4]{2,1,0:T(8,128)S(1)} %get-tuple-element.20.spread_ref) | copy-start | bytes 772
  (10 other events, 7.3 us)
